TPU v7x, 32 devices: a whole 2x2x4 slice. The times are simulated.
32 devices in a mesh: row: 8 (over z, x), col: 4 (over y, core).
Axes of the slice: x: 2, y: 2, z: 4, core: 2. Of those that a mesh axis runs over, the one named last changes fastest.
Arguments:
- grad: bfloat16 [16384, 1024], P(('row', 'col')), may hold values from -2500 to 2500
- left_root: bfloat16 [16384, 1024], P(('row', 'col')), may hold values from -0.051 to 3, as said below
- right_root: bfloat16 [16384, 1024], P(('row', 'col')), may hold values from -0.051 to 3, as said below
Outputs:
- update: bfloat16 [16384, 1024], P(('row', 'col'))
Inputs may be any that keep to these rules, and one draw needn't show every extreme that they name: `left_root`: each block L_b is symmetric and positive definite. `right_root`: each block R_b is symmetric and positive definite.
All inputs are finite; a program needn't handle non-finite values.
Results may differ from a plain program's by a relative error of at most 0.0049.
Values may be sent and summed in bfloat16 or wider, within the bound.
A program may use at most 64 MiB of HBM per device.

v0:
```python
import jax
import jax.numpy as jnp
from jax import lax
from jax.sharding import PartitionSpec as P

BLK = 1024
epsilon = 1e-06
clip_rms = 1.0


def partner(shard, axis, distance):
    return lax.ppermute(shard, axis, [(i, i ^ 1 << distance) for i in range(lax.axis_size(axis))])


def apply_right(gradient_rows, own_start, other_start, rows_here, right_root, partner_right):
    own_cols = lax.dynamic_slice_in_dim(gradient_rows, own_start, rows_here, 1)
    other_cols = lax.dynamic_slice_in_dim(gradient_rows, other_start, rows_here, 1)
    applied = jnp.dot(own_cols, right_root, preferred_element_type=jnp.float32)
    applied = applied + jnp.dot(other_cols, partner_right, preferred_element_type=jnp.float32)
    return applied.astype(jnp.bfloat16)


def shards(grad, left_root, right_root):
    rows_here = grad.shape[0]
    parity = lax.axis_index("col") % 2
    own_start = parity * rows_here
    other_start = (1 - parity) * rows_here
    partner_right = partner(right_root, "col", 0)
    right_applied = apply_right(grad, own_start, other_start, rows_here, right_root, partner_right)
    partner_rows = partner(right_applied, "col", 0)
    own_left = lax.dynamic_slice_in_dim(left_root, own_start, rows_here, 1)
    other_left = lax.dynamic_slice_in_dim(left_root, other_start, rows_here, 1)
    preconditioned = jnp.dot(own_left, right_applied, preferred_element_type=jnp.float32)
    preconditioned = preconditioned + jnp.dot(
        other_left, partner_rows, preferred_element_type=jnp.float32
    )
    grad_sq = jnp.sum(jnp.square(grad.astype(jnp.float32)))
    cond_sq = jnp.sum(preconditioned * preconditioned)
    global_sq = lax.psum(grad_sq, ("row", "col"))
    partner_sums = partner(jnp.stack([grad_sq, cond_sq]), "col", 0)
    block_grad = grad_sq + partner_sums[0]
    block_cond = cond_sq + partner_sums[1]
    block_count = BLK * BLK
    total_count = lax.axis_size("row") * lax.axis_size("col") // 2 * block_count
    clip_factor = clip_rms / jnp.sqrt(global_sq / total_count + epsilon)
    graft_ratio = jnp.sqrt(
        (block_grad / block_count + epsilon) / (block_cond / block_count + epsilon)
    )
    return (clip_factor * graft_ratio * preconditioned).astype(jnp.bfloat16)


def solution(mesh):
    placed = (P(("row", "col"), None), P(("row", "col"), None), P(("row", "col"), None))
    return jax.shard_map(
        shards, mesh=mesh, in_specs=placed, out_specs=P(("row", "col"), None), check_vma=False
    )
```

profile of v0, /device:TPU:0, one launch (start us, length us, event | category | flops | bytes accessed | tf_op | source)
XLA Modules:
  0.0 59.8 jit_solution(16291145906748680650)
XLA Ops:
  0.0 0.0 copy-start
  0.0 0.0 copy-start.1
  0.0 0.5 collective-permute-start
  0.5 2.1 %fusion.2 = f32[512,1024]{1,0:T(8,128)S(1)} fusion(bf16[512,1024]{1,0:T(8,128)(2,1)} %param.5, bf16[512,1024]{1,0:T(8,128)(2,1)} %param.3, s32[]{:T(128)S(6)} %select_n.16), kind=kOutput, calls=%fused_computation.7 | convolution fusion | flops 536870912 | bytes 3670020 | tf_op jit(solution)/shard_map/dot_general | solution.py:18
  2.6 0.5 collective-permute-done
  3.1 0.0 copy-done.1
  3.1 2.0 %add_convert_fusion = bf16[512,1024]{1,0:T(8,128)(2,1)S(1)} fusion(f32[512,1024]{1,0:T(8,128)S(1)} %fusion.2, bf16[512,1024]{1,0:T(8,128)(2,1)} %collective-permute-done, bf16[512,1024]{1,0:T(8,128)(2,1)S(1)} %copy-done.1, s32[]{:T(128)S(6)} %select_n.17), kind=kOutput, calls=%fused_computation.2 | convolution fusion | flops 537919488 | bytes 4718596 | tf_op jit(solution)/shard_map/dot_general | solution.py:19
  5.1 0.4 collective-permute-start.1
  5.5 1.2 %multiply_reduce_fusion.1 = f32[]{:T(128)} fusion(bf16[512,1024]{1,0:T(8,128)(2,1)S(1)} %copy-done.1), kind=kLoop, calls=%fused_computation.3 | loop fusion | flops 1572863 | bytes 1048580 | tf_op jit(solution)/shard_map/reduce_sum | solution.py:37
  6.7 41.8 %psum.7 = f32[]{:T(128)} all-reduce(f32[]{:T(128)} %multiply_reduce_fusion.1), channel_id=1, replica_groups=mesh['row'=8,'col'=4] {'row','col'}, use_global_device_ids=true, to_apply=%region_1.2 | all-reduce | flops 1 | bytes 8 | tf_op jit(solution)/shard_map/psum | solution.py:39
  49.3 0.0 copy-done
  49.3 0.7 %fusion.4 = f32[512,1024]{1,0:T(8,128)S(1)} fusion(bf16[512,1024]{1,0:T(8,128)(2,1)S(1)} %add_convert_fusion, bf16[512,1024]{1,0:T(8,128)(2,1)S(1)} %copy-done, s32[]{:T(128)S(6)} %select_n.16), kind=kOutput, calls=%fused_computation.9 | convolution fusion | flops 536870912 | bytes 3670020 | tf_op jit(solution)/shard_map/dot_general | solution.py:33
  50.0 0.0 collective-permute-done.1
  50.0 2.7 %multiply_reduce_fusion = (f32[]{:T(128)}, f32[512,1024]{1,0:T(8,128)S(1)}) fusion(f32[512,1024]{1,0:T(8,128)S(1)} %fusion.4, bf16[512,1024]{1,0:T(8,128)(2,1)} %collective-permute-done.1, bf16[512,1024]{1,0:T(8,128)(2,1)S(1)} %copy-done, s32[]{:T(128)S(6)} %select_n.17), kind=kOutput, calls=%fused_computation.1 | convolution fusion | flops 538443776 | bytes 5767176 | tf_op jit(solution)/shard_map/dot_general | solution.py:34
  52.7 1.4 %pad_maximum_fusion = f32[2]{0:T(128)S(1)} fusion(f32[1]{0:T(128)} %bitcast.1, f32[1]{0:T(128)} %bitcast), kind=kLoop, calls=%fused_computation.15 | loop fusion | flops 2 | bytes 16 | tf_op jit(solution)/shard_map/stack | solution.py:40
  54.1 0.0 collective-permute-start.2
  54.1 1.1 %collective-permute-done.2 = f32[2]{0:T(128)S(1)} collective-permute-done((f32[2]{0:T(128)S(1)}, f32[2]{0:T(128)S(1)}, u32[]{:S(2)}, u32[]{:S(2)}) %collective-permute-start.2) | collective-permute-done | bytes 40 | tf_op jit(solution)/shard_map/ppermute | solution.py:12
  55.3 0.7 %fusion.10 = (f32[1]{0:T(128)}, f32[1]{0:T(128)}) fusion(f32[2]{0:T(128)S(1)} %collective-permute-done.2), kind=kLoop, calls=%fused_computation.16 | loop fusion | bytes 16 | tf_op jit(solution)/shard_map/slice | solution.py:42
  58.6 1.2 %multiply_convert_fusion = bf16[512,1024]{1,0:T(8,128)(2,1)} fusion(f32[512,1024]{1,0:T(8,128)S(1)} %get-tuple-element.8, f32[]{:T(128)S(6)} %mul.21), kind=kLoop, calls=%fused_computation | loop fusion | flops 1048576 | bytes 3145732 | tf_op jit(solution)/shard_map/convert_element_type | solution.py:49
Async XLA Ops:
  0.0 49.3 %copy-start = (bf16[512,1024]{1,0:T(8,128)(2,1)S(1)}, bf16[512,1024]{1,0:T(8,128)(2,1)}, u32[]{:S(2)}) copy-start(bf16[512,1024]{1,0:T(8,128)(2,1)} %param.4) | copy-start | bytes 3145732
  0.0 3.1 %copy-start.1 = (bf16[512,1024]{1,0:T(8,128)(2,1)S(1)}, bf16[512,1024]{1,0:T(8,128)(2,1)}, u32[]{:S(2)}) copy-start(bf16[512,1024]{1,0:T(8,128)(2,1)} %param.3) | copy-start | bytes 3145732
  0.0 3.1 %collective-permute-start = (bf16[512,1024]{1,0:T(8,128)(2,1)}, bf16[512,1024]{1,0:T(8,128)(2,1)}, u32[]{:S(2)}, u32[]{:S(2)}) collective-permute-start(bf16[512,1024]{1,0:T(8,128)(2,1)} %param.5), channel_id=1, source_target_pairs={{0,1},{1,0},{2,3},{3,2},{4,5},{5,4},{6,7},{7,6},{8,9},{9,8},{10,11... | collective-permute-start | bytes 3145736 | tf_op jit(solution)/shard_map/ppermute | solution.py:12
  5.1 44.9 %collective-permute-start.1 = (bf16[512,1024]{1,0:T(8,128)(2,1)S(1)}, bf16[512,1024]{1,0:T(8,128)(2,1)}, u32[]{:S(2)}, u32[]{:S(2)}) collective-permute-start(bf16[512,1024]{1,0:T(8,128)(2,1)S(1)} %add_convert_fusion), channel_id=1, source_target_pairs={{0,1},{1,0},{2,3},{3,2},{4,5},{5,4},{6,7},{7,6},{8,9},{9,8},{10,11... | collective-permute-start | bytes 3145736 | tf_op jit(solution)/shard_map/ppermute | solution.py:12
  54.1 1.2 %collective-permute-start.2 = (f32[2]{0:T(128)S(1)}, f32[2]{0:T(128)S(1)}, u32[]{:S(2)}, u32[]{:S(2)}) collective-permute-start(f32[2]{0:T(128)S(1)} %pad_maximum_fusion), channel_id=1, source_target_pairs={{0,1},{1,0},{2,3},{3,2},{4,5},{5,4},{6,7},{7,6},{8,9},{9,8},{10,11... | collective-permute-start | bytes 32 | tf_op jit(solution)/shard_map/ppermute | solution.py:12
where the time goes:
time: 60.2 us; the launch traced here: 59.8 us
  blocking collectives  41.8 us (69%)
  matrix products  7.48 us (12%)
  other arithmetic  3.84 us (6%)
  between operations  3.42 us (6%)
  waiting for transfers between devices  1.68 us (3%)
  starting transfers between devices  0.94 us (2%)
  local copies, waits for them, and re-layouts  0.67 us (1%)
    psum x1, blocking collectives, shards(): global_sq = lax.psum(grad_sq, ('row', 'col'))  41.8 us
    dot_general x1, matrix products, shards(): jnp.dot(other_left, partner_rows, preferred_element_type=jnp.float32)  2.71 us
    dot_general x1, matrix products, apply_right(): applied = jnp.dot(own_cols, right_root, preferred_element_type=jnp.float32)  2.1 us
    dot_general x1, matrix products, apply_right(): jnp.dot(other_cols, partner_right, preferred_element_type=jnp.float32)  1.96 us
    ppermute x3, waiting for transfers between devices, partner(): lax.ppermute(shard, axis, [(i, i ^ 1 << distance) for i in range(lax.axis...  1.68 us
    another operation x1, other arithmetic, shards(): partner_sums = partner(jnp.stack([grad_sq, cond_sq]), 'col', 0)  1.41 us
    convert_element_type x1, other arithmetic, shards(): return (clip_factor * graft_ratio * preconditioned).astype(jnp.bfloat16)  1.22 us
    reduce_sum x1, other arithmetic, shards(): grad_sq = jnp.sum(jnp.square(grad.astype(jnp.float32)))  1.21 us
  transfers between devices with their start and end apart: 3, of which 2 were waited for; matrix products, arithmetic and copies ran while one was open for 7% of the time, Pallas kernels for 0%

commit v1 on v0

--- a/solution.py
+++ b/solution.py
@@ -36,7 +36,7 @@
     )
     grad_sq = jnp.sum(jnp.square(grad.astype(jnp.float32)))
     cond_sq = jnp.sum(preconditioned * preconditioned)
-    global_sq = lax.psum(grad_sq, ("row", "col"))
+    global_sq = lax.psum(lax.psum(grad_sq, "col"), "row")
     partner_sums = partner(jnp.stack([grad_sq, cond_sq]), "col", 0)
     block_grad = grad_sq + partner_sums[0]
     block_cond = cond_sq + partner_sums[1]

time: 60.2 us -> 49.5 us (0.82)
  blocking collectives: 41.8 us -> 31.1 us
    psum x1 -> x2, blocking collectives: 41.8 us -> 31.1 us  [shards(): global_sq = lax.psum(lax.psum(grad_sq, 'col'), 'row')]
  transfers between devices with their start and end apart: 3 -> 3, of which waited for: 2 -> 2; matrix products, arithmetic and copies ran while one was open for 7% -> 8% of each run, Pallas kernels for 0% -> 0%
where the time goes in v1:
time: 49.5 us; the launch traced here: 49.2 us
  blocking collectives  31.1 us (63%)
  matrix products  7.48 us (15%)
  other arithmetic  3.84 us (8%)
  between operations  3.42 us (7%)
  waiting for transfers between devices  1.68 us (3%)
  starting transfers between devices  0.94 us (2%)
  local copies, waits for them, and re-layouts  0.67 us (1%)
    psum x2, blocking collectives, shards(): global_sq = lax.psum(lax.psum(grad_sq, 'col'), 'row')  31.1 us
    dot_general x1, matrix products, shards(): jnp.dot(other_left, partner_rows, preferred_element_type=jnp.float32)  2.71 us
    dot_general x1, matrix products, apply_right(): applied = jnp.dot(own_cols, right_root, preferred_element_type=jnp.float32)  2.1 us
    dot_general x1, matrix products, apply_right(): jnp.dot(other_cols, partner_right, preferred_element_type=jnp.float32)  1.96 us
    ppermute x3, waiting for transfers between devices, partner(): lax.ppermute(shard, axis, [(i, i ^ 1 << distance) for i in range(lax.axis...  1.68 us
    another operation x1, other arithmetic, shards(): partner_sums = partner(jnp.stack([grad_sq, cond_sq]), 'col', 0)  1.41 us
    convert_element_type x1, other arithmetic, shards(): return (clip_factor * graft_ratio * preconditioned).astype(jnp.bfloat16)  1.22 us
    reduce_sum x1, other arithmetic, shards(): grad_sq = jnp.sum(jnp.square(grad.astype(jnp.float32)))  1.21 us
  transfers between devices with their start and end apart: 3, of which 2 were waited for; matrix products, arithmetic and copies ran while one was open for 8% of the time, Pallas kernels for 0%

profile of v1, /device:TPU:0, one launch (start us, length us, event | category | flops | bytes accessed | tf_op | source)
XLA Modules:
  0.0 49.2 jit_solution(11049162301493636608)
XLA Ops:
  0.0 0.0 copy-start
  0.0 0.0 copy-start.1
  0.0 0.5 %collective-permute-start = (bf16[512,1024]{1,0:T(8,128)(2,1)}, bf16[512,1024]{1,0:T(8,128)(2,1)}, u32[]{:S(2)}, u32[]{:S(2)}) collective-permute-start(bf16[512,1024]{1,0:T(8,128)(2,1)} %param.5), channel_id=1, source_target_pairs={{0,1},{1,0},{2,3},{3,2},{4,5},{5,4},{6,7},{7,6},{8,9},{9,8},{10,11... | collective-permute-start | bytes 3145736 | tf_op jit(solution)/shard_map/ppermute | solution.py:12
  0.5 2.1 %fusion.2 = f32[512,1024]{1,0:T(8,128)S(1)} fusion(bf16[512,1024]{1,0:T(8,128)(2,1)} %param.5, bf16[512,1024]{1,0:T(8,128)(2,1)} %param.3, s32[]{:T(128)S(6)} %select_n.16), kind=kOutput, calls=%fused_computation.7 | convolution fusion | flops 536870912 | bytes 3670020 | tf_op jit(solution)/shard_map/dot_general | solution.py:18
  2.6 0.5 %collective-permute-done = bf16[512,1024]{1,0:T(8,128)(2,1)} collective-permute-done((bf16[512,1024]{1,0:T(8,128)(2,1)}, bf16[512,1024]{1,0:T(8,128)(2,1)}, u32[]{:S(2)}, u32[]{:S(2)}) %collective-permute-start) | collective-permute-done | bytes 1048608 | tf_op jit(solution)/shard_map/ppermute | solution.py:12
  3.1 0.0 copy-done.1
  3.1 2.0 %add_convert_fusion = bf16[512,1024]{1,0:T(8,128)(2,1)S(1)} fusion(f32[512,1024]{1,0:T(8,128)S(1)} %fusion.2, bf16[512,1024]{1,0:T(8,128)(2,1)} %collective-permute-done, bf16[512,1024]{1,0:T(8,128)(2,1)S(1)} %copy-done.1, s32[]{:T(128)S(6)} %select_n.17), kind=kOutput, calls=%fused_computation.2 | convolution fusion | flops 537919488 | bytes 4718596 | tf_op jit(solution)/shard_map/dot_general | solution.py:19
  5.1 0.4 collective-permute-start.1
  5.5 1.2 %multiply_reduce_fusion.1 = f32[]{:T(128)} fusion(bf16[512,1024]{1,0:T(8,128)(2,1)S(1)} %copy-done.1), kind=kLoop, calls=%fused_computation.3 | loop fusion | flops 1572863 | bytes 1048580 | tf_op jit(solution)/shard_map/reduce_sum | solution.py:37
  6.7 8.9 %psum.14 = f32[]{:T(128)} all-reduce(f32[]{:T(128)} %multiply_reduce_fusion.1), channel_id=1, replica_groups=mesh['row'=8,'col'=4] {'col'}, use_global_device_ids=true, to_apply=%region_1.2 | all-reduce | flops 1 | bytes 8 | tf_op jit(solution)/shard_map/psum | solution.py:39
  15.6 22.3 %psum.15 = f32[]{:T(128)} all-reduce(f32[]{:T(128)} %psum.14), channel_id=1, replica_groups=mesh['row'=8,'col'=4] {'row'}, use_global_device_ids=true, to_apply=%region_2.3 | all-reduce | flops 1 | bytes 8 | tf_op jit(solution)/shard_map/psum | solution.py:39
  38.6 0.0 copy-done
  38.6 0.7 %fusion.4 = f32[512,1024]{1,0:T(8,128)S(1)} fusion(bf16[512,1024]{1,0:T(8,128)(2,1)S(1)} %add_convert_fusion, bf16[512,1024]{1,0:T(8,128)(2,1)S(1)} %copy-done, s32[]{:T(128)S(6)} %select_n.16), kind=kOutput, calls=%fused_computation.9 | convolution fusion | flops 536870912 | bytes 3670020 | tf_op jit(solution)/shard_map/dot_general | solution.py:33
  39.3 0.0 collective-permute-done.1
  39.3 2.7 %multiply_reduce_fusion = (f32[]{:T(128)}, f32[512,1024]{1,0:T(8,128)S(1)}) fusion(f32[512,1024]{1,0:T(8,128)S(1)} %fusion.4, bf16[512,1024]{1,0:T(8,128)(2,1)} %collective-permute-done.1, bf16[512,1024]{1,0:T(8,128)(2,1)S(1)} %copy-done, s32[]{:T(128)S(6)} %select_n.17), kind=kOutput, calls=%fused_computation.1 | convolution fusion | flops 538443776 | bytes 5767176 | tf_op jit(solution)/shard_map/dot_general | solution.py:34
  42.0 1.4 %pad_maximum_fusion = f32[2]{0:T(128)S(1)} fusion(f32[1]{0:T(128)} %bitcast.1, f32[1]{0:T(128)} %bitcast), kind=kLoop, calls=%fused_computation.15 | loop fusion | flops 2 | bytes 16 | tf_op jit(solution)/shard_map/stack | solution.py:40
  43.4 0.0 collective-permute-start.2
  43.5 1.1 %collective-permute-done.2 = f32[2]{0:T(128)S(1)} collective-permute-done((f32[2]{0:T(128)S(1)}, f32[2]{0:T(128)S(1)}, u32[]{:S(2)}, u32[]{:S(2)}) %collective-permute-start.2) | collective-permute-done | bytes 40 | tf_op jit(solution)/shard_map/ppermute | solution.py:12
  44.6 0.7 %fusion.10 = (f32[1]{0:T(128)}, f32[1]{0:T(128)}) fusion(f32[2]{0:T(128)S(1)} %collective-permute-done.2), kind=kLoop, calls=%fused_computation.16 | loop fusion | bytes 16 | tf_op jit(solution)/shard_map/slice | solution.py:42
  47.9 1.2 %multiply_convert_fusion = bf16[512,1024]{1,0:T(8,128)(2,1)} fusion(f32[512,1024]{1,0:T(8,128)S(1)} %get-tuple-element.8, f32[]{:T(128)S(6)} %mul.21), kind=kLoop, calls=%fused_computation | loop fusion | flops 1048576 | bytes 3145732 | tf_op jit(solution)/shard_map/convert_element_type | solution.py:49
Async XLA Ops:
  0.0 38.6 %copy-start = (bf16[512,1024]{1,0:T(8,128)(2,1)S(1)}, bf16[512,1024]{1,0:T(8,128)(2,1)}, u32[]{:S(2)}) copy-start(bf16[512,1024]{1,0:T(8,128)(2,1)} %param.4) | copy-start | bytes 3145732
  0.0 3.1 %copy-start.1 = (bf16[512,1024]{1,0:T(8,128)(2,1)S(1)}, bf16[512,1024]{1,0:T(8,128)(2,1)}, u32[]{:S(2)}) copy-start(bf16[512,1024]{1,0:T(8,128)(2,1)} %param.3) | copy-start | bytes 3145732
  0.0 3.1 %collective-permute-start = (bf16[512,1024]{1,0:T(8,128)(2,1)}, bf16[512,1024]{1,0:T(8,128)(2,1)}, u32[]{:S(2)}, u32[]{:S(2)}) collective-permute-start(bf16[512,1024]{1,0:T(8,128)(2,1)} %param.5), channel_id=1, source_target_pairs={{0,1},{1,0},{2,3},{3,2},{4,5},{5,4},{6,7},{7,6},{8,9},{9,8},{10,11... | collective-permute-start | bytes 3145736 | tf_op jit(solution)/shard_map/ppermute | solution.py:12
  5.1 34.2 %collective-permute-start.1 = (bf16[512,1024]{1,0:T(8,128)(2,1)S(1)}, bf16[512,1024]{1,0:T(8,128)(2,1)}, u32[]{:S(2)}, u32[]{:S(2)}) collective-permute-start(bf16[512,1024]{1,0:T(8,128)(2,1)S(1)} %add_convert_fusion), channel_id=1, source_target_pairs={{0,1},{1,0},{2,3},{3,2},{4,5},{5,4},{6,7},{7,6},{8,9},{9,8},{10,11... | collective-permute-start | bytes 3145736 | tf_op jit(solution)/shard_map/ppermute | solution.py:12
  43.4 1.2 %collective-permute-start.2 = (f32[2]{0:T(128)S(1)}, f32[2]{0:T(128)S(1)}, u32[]{:S(2)}, u32[]{:S(2)}) collective-permute-start(f32[2]{0:T(128)S(1)} %pad_maximum_fusion), channel_id=1, source_target_pairs={{0,1},{1,0},{2,3},{3,2},{4,5},{5,4},{6,7},{7,6},{8,9},{9,8},{10,11... | collective-permute-start | bytes 32 | tf_op jit(solution)/shard_map/ppermute | solution.py:12
